TPU v7x, 32 devices: a whole 2x2x4 slice. The times are simulated.
32 devices in a mesh: prow: 8 (over y, x, core), pcol: 4 (over z).
Axes of the slice: x: 2, y: 2, z: 4, core: 2. Of those that a mesh axis runs over, the one named last changes fastest.
Arguments:
- rhs: bfloat16 [128, 64, 256], P('prow'), may hold values from -6 to 6
- blocks: bfloat16 [128, 16, 256, 256], P('prow', 'pcol'), may hold values from -0.0625 to 0.0625
- inverses: bfloat16 [128, 256, 256], P('prow'), may hold values from -1 to 2.1, as said below
- columns: int32 [128, 16], P('prow', 'pcol'), may hold values from 0 to 127, as said below
- counts: int32 [128, 4], P('prow', 'pcol'), may hold values from 0 to 4, as said below
Outputs:
- solved: bfloat16 [128, 64, 256], P('prow')
Inputs may be any that keep to these rules, and one draw needn't show every extreme that they name: `columns`: slot c of array row o names a block row k (level order) of an earlier level than that of o, with (k // 8) % 4 == c // 4, or 0 where no such block row exists; only the first counts[o, c // 4] slots of a group are used. `counts`: 0 where the group has no earlier block row (level 0 in particular); otherwise 1 or more. `inverses`: each tile is the inverse of a lower triangular diagonal block, itself lower triangular.
All inputs are finite; a program needn't handle non-finite values.
Results may differ from a plain program's by a relative error of at most 0.0054.
Values may be sent and summed in bfloat16 or wider, within the bound.
No kernel may reach another device: no remote copies, remote signals or barrier semaphores. Data moves between devices by JAX's collectives and lax.ppermute only.
A program may use at most 64 MiB of HBM per device.

v0:
```python
import jax
import jax.numpy as jnp
from jax import lax
from jax.sharding import PartitionSpec as P

LEVELS = 8
LR = 2


def body(rhs, blocks, inverses, columns, counts):
    side_count = rhs.shape[1]
    block_size = rhs.shape[2]
    prow_count = lax.axis_size("prow")
    pcol_count = lax.axis_size("pcol")
    per_level = LR * prow_count
    slot_count = columns.shape[1]
    active_mask = (jnp.arange(slot_count, dtype=jnp.int32)[None, :] < counts).astype(jnp.bfloat16)
    store_rows = LEVELS * prow_count
    solved_store = jnp.zeros((store_rows, side_count, block_size), jnp.bfloat16)
    solution = jnp.zeros(rhs.shape, jnp.bfloat16)

    def advance(level_no, carry):
        solved_store, solution = carry
        first_row = level_no * LR
        column_ids = lax.dynamic_slice_in_dim(columns, first_row, LR, 0)
        active = lax.dynamic_slice_in_dim(active_mask, first_row, LR, 0)
        panels = lax.dynamic_slice_in_dim(blocks, first_row, LR, 0)
        right_side = lax.dynamic_slice_in_dim(rhs, first_row, LR, 0)
        inverse_tiles = lax.dynamic_slice_in_dim(inverses, first_row, LR, 0)
        store_ids = column_ids // per_level * prow_count + column_ids % prow_count
        gathered = jnp.take(solved_store, store_ids, axis=0) * active[:, :, None, None]
        update_sum = jnp.einsum(
            "scrj,scij->sri", gathered, panels, preferred_element_type=jnp.float32
        )
        which_half = (lax.axis_index("pcol") - level_no * LR) % pcol_count
        keep_half = (which_half < LR).astype(jnp.bfloat16)
        half_index = jnp.minimum(which_half, LR - 1)
        summed = lax.psum(update_sum, "pcol")
        residual = (right_side.astype(jnp.float32) - summed).astype(jnp.bfloat16)
        solved_now = jnp.einsum(
            "srb,sab->sra", residual, inverse_tiles, preferred_element_type=jnp.float32
        ).astype(jnp.bfloat16)
        payload = lax.dynamic_index_in_dim(solved_now, half_index, 0, keepdims=True) * keep_half
        level_block = lax.all_gather(payload[None], "prow", axis=0, tiled=True)
        column_block = level_block.reshape((prow_count, side_count, block_size))
        solved_store = lax.dynamic_update_slice_in_dim(
            solved_store, column_block, level_no * prow_count, 0
        )
        solution = lax.dynamic_update_slice_in_dim(solution, solved_now, first_row, 0)
        return (solved_store, solution)

    solved_store, solution = lax.fori_loop(0, LEVELS, advance, (solved_store, solution))
    return solution


def solution(mesh):
    placed = (
        P("prow", None, None),
        P("prow", "pcol", None, None),
        P("prow", None, None),
        P("prow", "pcol"),
        P("prow", "pcol"),
    )
    return jax.shard_map(
        body, mesh=mesh, in_specs=placed, out_specs=P("prow", None, None), check_vma=False
    )
```

profile of v0, /device:TPU:0, one launch (start us, length us, event | category | flops | bytes accessed | tf_op | source)
XLA Modules:
  0.0 398.1 jit_solution(2024207592908420231)
XLA Ops:
  8.3 382.1 %while.18 = (s32[]{:T(128)}, bf16[64,64,256]{2,1,0:T(8,128)(2,1)S(1)}, bf16[16,64,256]{2,1,0:T(8,128)(2,1)S(1)}, bf16[16,64,256]{2,1,0:T(8,128)(2,1)}, s32[16,4]...) while((s32[]{:T(128)}, ...), condition=%wide.region_2.3_spmd, body=%wide.region_0.2_spmd.sunk | while | flops 84329728 | bytes 4233478 | solution.py:52
  9.1 2.3 convolution_bitcast_fusion.2
  11.5 37.5 %all-reduce.2.cloned.1.call-done = f32[2,64,256]{2,1,0:T(8,128)} async-done(((f32[2,64,256]{2,1,0:T(8,128)}), f32[2,64,256]{2,1,0:T(8,128)}) %all-reduce.2.cloned.1.call-update) | async-done | bytes 131088 | tf_op jit(solution)/shard_map/while/body/eval_jaxpr/psum | solution.py:38
  49.0 1.3 constant_dynamic-update-slice_fusion.4
  50.2 9.2 %all-gather.2 = bf16[8,64,256]{2,1,0:T(8,128)(2,1)S(1)} all-gather(bf16[1,64,256]{2,1,0:T(8,128)(2,1)S(1)} %dynamic-slice_multiply_fusion.2), channel_id=2, replica_groups=mesh['prow'=8,'pcol'=4] {'prow'}, dimensions={0}, use_global_device_ids=true | all-gather | bytes 294912 | tf_op jit(solution)/shard_map/while/body/eval_jaxpr/all_gather | solution.py:44
  60.3 2.3 convolution_bitcast_fusion.2
  62.7 33.6 %all-reduce.2.cloned.1.call-done = f32[2,64,256]{2,1,0:T(8,128)} async-done(((f32[2,64,256]{2,1,0:T(8,128)}), f32[2,64,256]{2,1,0:T(8,128)}) %all-reduce.2.cloned.1.call-update) | async-done | bytes 131088 | tf_op jit(solution)/shard_map/while/body/eval_jaxpr/psum | solution.py:38
  96.2 1.3 constant_dynamic-update-slice_fusion.4
  97.5 9.2 %all-gather.2 = bf16[8,64,256]{2,1,0:T(8,128)(2,1)S(1)} all-gather(bf16[1,64,256]{2,1,0:T(8,128)(2,1)S(1)} %dynamic-slice_multiply_fusion.2), channel_id=2, replica_groups=mesh['prow'=8,'pcol'=4] {'prow'}, dimensions={0}, use_global_device_ids=true | all-gather | bytes 294912 | tf_op jit(solution)/shard_map/while/body/eval_jaxpr/all_gather | solution.py:44
  107.6 2.3 convolution_bitcast_fusion.2
  110.0 33.5 %all-reduce.2.cloned.1.call-done = f32[2,64,256]{2,1,0:T(8,128)} async-done(((f32[2,64,256]{2,1,0:T(8,128)}), f32[2,64,256]{2,1,0:T(8,128)}) %all-reduce.2.cloned.1.call-update) | async-done | bytes 131088 | tf_op jit(solution)/shard_map/while/body/eval_jaxpr/psum | solution.py:38
  143.5 1.3 constant_dynamic-update-slice_fusion.4
  144.8 9.2 %all-gather.2 = bf16[8,64,256]{2,1,0:T(8,128)(2,1)S(1)} all-gather(bf16[1,64,256]{2,1,0:T(8,128)(2,1)S(1)} %dynamic-slice_multiply_fusion.2), channel_id=2, replica_groups=mesh['prow'=8,'pcol'=4] {'prow'}, dimensions={0}, use_global_device_ids=true | all-gather | bytes 294912 | tf_op jit(solution)/shard_map/while/body/eval_jaxpr/all_gather | solution.py:44
  154.8 2.3 convolution_bitcast_fusion.2
  157.2 33.5 %all-reduce.2.cloned.1.call-done = f32[2,64,256]{2,1,0:T(8,128)} async-done(((f32[2,64,256]{2,1,0:T(8,128)}), f32[2,64,256]{2,1,0:T(8,128)}) %all-reduce.2.cloned.1.call-update) | async-done | bytes 131088 | tf_op jit(solution)/shard_map/while/body/eval_jaxpr/psum | solution.py:38
  190.8 1.3 constant_dynamic-update-slice_fusion.4
  192.1 9.2 %all-gather.2 = bf16[8,64,256]{2,1,0:T(8,128)(2,1)S(1)} all-gather(bf16[1,64,256]{2,1,0:T(8,128)(2,1)S(1)} %dynamic-slice_multiply_fusion.2), channel_id=2, replica_groups=mesh['prow'=8,'pcol'=4] {'prow'}, dimensions={0}, use_global_device_ids=true | all-gather | bytes 294912 | tf_op jit(solution)/shard_map/while/body/eval_jaxpr/all_gather | solution.py:44
  202.1 2.3 convolution_bitcast_fusion.2
  204.5 33.5 %all-reduce.2.cloned.1.call-done = f32[2,64,256]{2,1,0:T(8,128)} async-done(((f32[2,64,256]{2,1,0:T(8,128)}), f32[2,64,256]{2,1,0:T(8,128)}) %all-reduce.2.cloned.1.call-update) | async-done | bytes 131088 | tf_op jit(solution)/shard_map/while/body/eval_jaxpr/psum | solution.py:38
  238.1 1.3 constant_dynamic-update-slice_fusion.4
  239.3 9.2 %all-gather.2 = bf16[8,64,256]{2,1,0:T(8,128)(2,1)S(1)} all-gather(bf16[1,64,256]{2,1,0:T(8,128)(2,1)S(1)} %dynamic-slice_multiply_fusion.2), channel_id=2, replica_groups=mesh['prow'=8,'pcol'=4] {'prow'}, dimensions={0}, use_global_device_ids=true | all-gather | bytes 294912 | tf_op jit(solution)/shard_map/while/body/eval_jaxpr/all_gather | solution.py:44
  249.4 2.3 convolution_bitcast_fusion.2
  251.8 33.5 %all-reduce.2.cloned.1.call-done = f32[2,64,256]{2,1,0:T(8,128)} async-done(((f32[2,64,256]{2,1,0:T(8,128)}), f32[2,64,256]{2,1,0:T(8,128)}) %all-reduce.2.cloned.1.call-update) | async-done | bytes 131088 | tf_op jit(solution)/shard_map/while/body/eval_jaxpr/psum | solution.py:38
  285.3 1.3 constant_dynamic-update-slice_fusion.4
  286.6 9.2 %all-gather.2 = bf16[8,64,256]{2,1,0:T(8,128)(2,1)S(1)} all-gather(bf16[1,64,256]{2,1,0:T(8,128)(2,1)S(1)} %dynamic-slice_multiply_fusion.2), channel_id=2, replica_groups=mesh['prow'=8,'pcol'=4] {'prow'}, dimensions={0}, use_global_device_ids=true | all-gather | bytes 294912 | tf_op jit(solution)/shard_map/while/body/eval_jaxpr/all_gather | solution.py:44
  296.7 2.3 convolution_bitcast_fusion.2
  299.1 33.5 %all-reduce.2.cloned.1.call-done = f32[2,64,256]{2,1,0:T(8,128)} async-done(((f32[2,64,256]{2,1,0:T(8,128)}), f32[2,64,256]{2,1,0:T(8,128)}) %all-reduce.2.cloned.1.call-update) | async-done | bytes 131088 | tf_op jit(solution)/shard_map/while/body/eval_jaxpr/psum | solution.py:38
  333.9 9.2 %all-gather.2 = bf16[8,64,256]{2,1,0:T(8,128)(2,1)S(1)} all-gather(bf16[1,64,256]{2,1,0:T(8,128)(2,1)S(1)} %dynamic-slice_multiply_fusion.2), channel_id=2, replica_groups=mesh['prow'=8,'pcol'=4] {'prow'}, dimensions={0}, use_global_device_ids=true | all-gather | bytes 294912 | tf_op jit(solution)/shard_map/while/body/eval_jaxpr/all_gather | solution.py:44
  343.9 2.3 convolution_bitcast_fusion.2
  346.4 33.5 %all-reduce.2.cloned.1.call-done = f32[2,64,256]{2,1,0:T(8,128)} async-done(((f32[2,64,256]{2,1,0:T(8,128)}), f32[2,64,256]{2,1,0:T(8,128)}) %all-reduce.2.cloned.1.call-update) | async-done | bytes 131088 | tf_op jit(solution)/shard_map/while/body/eval_jaxpr/psum | solution.py:38
  379.9 1.3 constant_dynamic-update-slice_fusion.4
  381.2 9.2 %all-gather.2 = bf16[8,64,256]{2,1,0:T(8,128)(2,1)S(1)} all-gather(bf16[1,64,256]{2,1,0:T(8,128)(2,1)S(1)} %dynamic-slice_multiply_fusion.2), channel_id=2, replica_groups=mesh['prow'=8,'pcol'=4] {'prow'}, dimensions={0}, use_global_device_ids=true | all-gather | bytes 294912 | tf_op jit(solution)/shard_map/while/body/eval_jaxpr/all_gather | solution.py:44
  (79 shorter events, 10.1 us)
Async XLA Ops:
  8.3 40.6 %all-reduce.2.cloned.1.call-start = ((), (), s32[]{:S(2)}) async-start(), calls=%async_computation | async-start | bytes 262144 | tf_op jit(solution)/shard_map/while/body/eval_jaxpr/psum | solution.py:38
  59.5 36.7 %all-reduce.2.cloned.1.call-start = ((), (), s32[]{:S(2)}) async-start(), calls=%async_computation | async-start | bytes 262144 | tf_op jit(solution)/shard_map/while/body/eval_jaxpr/psum | solution.py:38
  106.8 36.7 %all-reduce.2.cloned.1.call-start = ((), (), s32[]{:S(2)}) async-start(), calls=%async_computation | async-start | bytes 262144 | tf_op jit(solution)/shard_map/while/body/eval_jaxpr/psum | solution.py:38
  154.1 36.7 %all-reduce.2.cloned.1.call-start = ((), (), s32[]{:S(2)}) async-start(), calls=%async_computation | async-start | bytes 262144 | tf_op jit(solution)/shard_map/while/body/eval_jaxpr/psum | solution.py:38
  201.4 36.7 %all-reduce.2.cloned.1.call-start = ((), (), s32[]{:S(2)}) async-start(), calls=%async_computation | async-start | bytes 262144 | tf_op jit(solution)/shard_map/while/body/eval_jaxpr/psum | solution.py:38
  248.6 36.7 %all-reduce.2.cloned.1.call-start = ((), (), s32[]{:S(2)}) async-start(), calls=%async_computation | async-start | bytes 262144 | tf_op jit(solution)/shard_map/while/body/eval_jaxpr/psum | solution.py:38
  295.9 36.7 %all-reduce.2.cloned.1.call-start = ((), (), s32[]{:S(2)}) async-start(), calls=%async_computation | async-start | bytes 262144 | tf_op jit(solution)/shard_map/while/body/eval_jaxpr/psum | solution.py:38
  343.2 36.7 %all-reduce.2.cloned.1.call-start = ((), (), s32[]{:S(2)}) async-start(), calls=%async_computation | async-start | bytes 262144 | tf_op jit(solution)/shard_map/while/body/eval_jaxpr/psum | solution.py:38
  390.4 0.8 copy-start
Sparse Core Ops, SparseCore 0:
  11.6 37.3 all-reduce.1
  62.8 33.4 all-reduce.1
  110.1 33.4 all-reduce.1
  157.3 33.4 all-reduce.1
  204.6 33.4 all-reduce.1
  251.9 33.4 all-reduce.1
  299.2 33.4 all-reduce.1
  346.4 33.4 all-reduce.1
where the time goes:
time: 399 us; the launch traced here: 398 us
  waiting for transfers between devices  272 us (68%)
  blocking collectives  74 us (19%)
  matrix products  28.7 us (7%)
  between operations  13.4 us (3%)
  local copies, waits for them, and re-layouts  7.25 us (2%)
    psum x8, waiting for transfers between devices, advance(): summed = lax.psum(update_sum, 'pcol')  272 us
    all_gather x8, blocking collectives, advance(): level_block = lax.all_gather(payload[None], 'prow', axis=0, tiled=True)  74 us
    dot_general x8, matrix products, advance(): jnp.einsum('scrj,scij->sri', gathered, panels, preferred_element_type=jnp...  18.7 us
    dot_general x8, matrix products, advance(): jnp.einsum('srb,sab->sra', residual, inverse_tiles, preferred_element_typ...  10 us
  transfers between devices with their start and end apart: 8, of which 8 were waited for; matrix products, arithmetic and copies ran while one was open for 0% of the time, Pallas kernels for 0%

commit v1 on v0

--- a/solution.py
+++ b/solution.py
@@ -35,7 +35,14 @@
         which_half = (lax.axis_index("pcol") - level_no * LR) % pcol_count
         keep_half = (which_half < LR).astype(jnp.bfloat16)
         half_index = jnp.minimum(which_half, LR - 1)
-        summed = lax.psum(update_sum, "pcol")
+        n_parts = jax.lax.axis_size("pcol")
+        summed, ready = (update_sum, 0)
+        while 1 << ready < n_parts:
+            y_new = jax.lax.ppermute(
+                summed, axis_name="pcol", perm=[(kk, kk ^ 1 << ready) for kk in range(n_parts)]
+            )
+            summed = summed + y_new
+            ready = ready + 1
         residual = (right_side.astype(jnp.float32) - summed).astype(jnp.bfloat16)
         solved_now = jnp.einsum(
             "srb,sab->sra", residual, inverse_tiles, preferred_element_type=jnp.float32

time: 399 us -> 220 us (0.55)
  waiting for transfers between devices: 272 us -> 88.7 us
  starting transfers between devices: 0.33 us -> 27.7 us
  between operations: 13.4 us -> 0.03 us
  matrix products: 28.7 us -> 22.9 us
    psum x8 -> x0, waiting for transfers between devices: 272 us -> none  [advance(): summed = lax.psum(update_sum, 'pcol')]
    ppermute x0 -> x16, waiting for transfers between devices: none -> 88.7 us  [advance(): jax.lax.ppermute(summed, axis_name='pcol', perm=[(kk, kk ^ 1 << ready) fo...]
    ppermute x0 -> x16, starting transfers between devices: none -> 27.7 us  [advance(): jax.lax.ppermute(summed, axis_name='pcol', perm=[(kk, kk ^ 1 << ready) fo...]
    dot_general x8, matrix products: 18.7 us -> 13.4 us  [advance(): jnp.einsum('scrj,scij->sri', gathered, panels, preferred_element_type=jnp...]
  transfers between devices with their start and end apart: 8 -> 16, of which waited for: 8 -> 16; matrix products, arithmetic and copies ran while one was open for 0% -> 0% of each run, Pallas kernels for 0% -> 0%
where the time goes in v1:
time: 220 us
  waiting for transfers between devices  88.7 us (40%)
  blocking collectives  71.3 us (32%)
  starting transfers between devices  27.7 us (13%)
  matrix products  22.9 us (10%)
  local copies, waits for them, and re-layouts  7.25 us (3%)
    ppermute x16, waiting for transfers between devices, advance(): jax.lax.ppermute(summed, axis_name='pcol', perm=[(kk, kk ^ 1 << ready) fo...  88.7 us
    all_gather x8, blocking collectives, advance(): level_block = lax.all_gather(payload[None], 'prow', axis=0, tiled=True)  71.3 us
    ppermute x16, starting transfers between devices, advance(): jax.lax.ppermute(summed, axis_name='pcol', perm=[(kk, kk ^ 1 << ready) fo...  27.7 us
    dot_general x8, matrix products, advance(): jnp.einsum('scrj,scij->sri', gathered, panels, preferred_element_type=jnp...  13.4 us
    dot_general x8, matrix products, advance(): jnp.einsum('srb,sab->sra', residual, inverse_tiles, preferred_element_typ...  9.53 us
    gather x8, local copies, waits for them, and re-layouts, advance(): jnp.take(solved_store, store_ids, axis=0) * active[:, :, None, None]  4.5 us
  transfers between devices with their start and end apart: 16, of which 16 were waited for; matrix products, arithmetic and copies ran while one was open for 0% of the time, Pallas kernels for 0%

profile of v1, /device:TPU:0, one launch (start us, length us, event | category | flops | bytes accessed | tf_op | source)
XLA Modules:
  0.0 219.7 jit_solution(13621038159217790067)
XLA Ops:
  1.8 217.1 %while.18 = (s32[]{:T(128)}, bf16[64,64,256]{2,1,0:T(8,128)(2,1)S(1)}, bf16[16,64,256]{2,1,0:T(8,128)(2,1)S(1)}, bf16[16,64,256]{2,1,0:T(8,128)(2,1)}, s32[16,4]...) while((s32[]{:T(128)}, ...), condition=%wide.region_1.2_spmd, body=%wide.region_0.1_spmd.sunk | while | flops 84362496 | bytes 5019950 | solution.py:59
  4.2 3.1 %collective-permute-start = (f32[2,64,256]{2,1,0:T(8,128)S(1)}, f32[2,64,256]{2,1,0:T(8,128)S(1)}, u32[]{:S(2)}, u32[]{:S(2)}) collective-permute-start(f32[2,64,256]{2,1,0:T(8,128)S(1)} %convolution_bitcast_fusion.2), channel_id=1, source_target_pairs={{0,1},{1,0},{2,3},{3,2},{4,5},{5,4},{6,7},{7,6},{8,9},{9,8},{10,11... | collective-permute-start | bytes 393224 | tf_op jit(solution)/shard_map/while/body/eval_jaxpr/ppermute | solution.py:41
  7.3 3.5 %collective-permute-done = f32[2,64,256]{2,1,0:T(8,128)S(1)} collective-permute-done((f32[2,64,256]{2,1,0:T(8,128)S(1)}, f32[2,64,256]{2,1,0:T(8,128)S(1)}, u32[]{:S(2)}, u32[]{:S(2)}) %collective-permute-start) | collective-permute-done | bytes 131104 | tf_op jit(solution)/shard_map/while/body/eval_jaxpr/ppermute | solution.py:41
  10.8 2.8 %collective-permute-start.1 = (f32[2,64,256]{2,1,0:T(8,128)S(1)}, f32[2,64,256]{2,1,0:T(8,128)S(1)}, u32[]{:S(2)}, u32[]{:S(2)}) collective-permute-start(f32[2,64,256]{2,1,0:T(8,128)S(1)} %add.164), channel_id=1, source_target_pairs={{0,2},{1,3},{2,0},{3,1},{4,6},{5,7},{6,4},{7,5},{8,10},{9,11},{10,... | collective-permute-start | bytes 393224 | tf_op jit(solution)/shard_map/while/body/eval_jaxpr/ppermute | solution.py:41
  13.7 5.6 %collective-permute-done.1 = f32[2,64,256]{2,1,0:T(8,128)S(1)} collective-permute-done((f32[2,64,256]{2,1,0:T(8,128)S(1)}, f32[2,64,256]{2,1,0:T(8,128)S(1)}, u32[]{:S(2)}, u32[]{:S(2)}) %collective-permute-start.1) | collective-permute-done | bytes 131104 | tf_op jit(solution)/shard_map/while/body/eval_jaxpr/ppermute | solution.py:41
  20.5 9.2 %all-gather.2 = bf16[8,64,256]{2,1,0:T(8,128)(2,1)S(1)} all-gather(bf16[1,64,256]{2,1,0:T(8,128)(2,1)S(1)} %dynamic-slice_multiply_fusion.2), channel_id=2, replica_groups=mesh['prow'=8,'pcol'=4] {'prow'}, dimensions={0}, use_global_device_ids=true | all-gather | bytes 294912 | tf_op jit(solution)/shard_map/while/body/eval_jaxpr/all_gather | solution.py:51
  32.8 5.1 %collective-permute-done = f32[2,64,256]{2,1,0:T(8,128)S(1)} collective-permute-done((f32[2,64,256]{2,1,0:T(8,128)S(1)}, f32[2,64,256]{2,1,0:T(8,128)S(1)}, u32[]{:S(2)}, u32[]{:S(2)}) %collective-permute-start) | collective-permute-done | bytes 131104 | tf_op jit(solution)/shard_map/while/body/eval_jaxpr/ppermute | solution.py:41
  37.9 2.4 %collective-permute-start.1 = (f32[2,64,256]{2,1,0:T(8,128)S(1)}, f32[2,64,256]{2,1,0:T(8,128)S(1)}, u32[]{:S(2)}, u32[]{:S(2)}) collective-permute-start(f32[2,64,256]{2,1,0:T(8,128)S(1)} %add.164), channel_id=1, source_target_pairs={{0,2},{1,3},{2,0},{3,1},{4,6},{5,7},{6,4},{7,5},{8,10},{9,11},{10,... | collective-permute-start | bytes 393224 | tf_op jit(solution)/shard_map/while/body/eval_jaxpr/ppermute | solution.py:41
  40.3 6.3 %collective-permute-done.1 = f32[2,64,256]{2,1,0:T(8,128)S(1)} collective-permute-done((f32[2,64,256]{2,1,0:T(8,128)S(1)}, f32[2,64,256]{2,1,0:T(8,128)S(1)}, u32[]{:S(2)}, u32[]{:S(2)}) %collective-permute-start.1) | collective-permute-done | bytes 131104 | tf_op jit(solution)/shard_map/while/body/eval_jaxpr/ppermute | solution.py:41
  47.8 9.3 %all-gather.2 = bf16[8,64,256]{2,1,0:T(8,128)(2,1)S(1)} all-gather(bf16[1,64,256]{2,1,0:T(8,128)(2,1)S(1)} %dynamic-slice_multiply_fusion.2), channel_id=2, replica_groups=mesh['prow'=8,'pcol'=4] {'prow'}, dimensions={0}, use_global_device_ids=true | all-gather | bytes 294912 | tf_op jit(solution)/shard_map/while/body/eval_jaxpr/all_gather | solution.py:51
  60.3 5.1 %collective-permute-done = f32[2,64,256]{2,1,0:T(8,128)S(1)} collective-permute-done((f32[2,64,256]{2,1,0:T(8,128)S(1)}, f32[2,64,256]{2,1,0:T(8,128)S(1)}, u32[]{:S(2)}, u32[]{:S(2)}) %collective-permute-start) | collective-permute-done | bytes 131104 | tf_op jit(solution)/shard_map/while/body/eval_jaxpr/ppermute | solution.py:41
  65.4 2.4 %collective-permute-start.1 = (f32[2,64,256]{2,1,0:T(8,128)S(1)}, f32[2,64,256]{2,1,0:T(8,128)S(1)}, u32[]{:S(2)}, u32[]{:S(2)}) collective-permute-start(f32[2,64,256]{2,1,0:T(8,128)S(1)} %add.164), channel_id=1, source_target_pairs={{0,2},{1,3},{2,0},{3,1},{4,6},{5,7},{6,4},{7,5},{8,10},{9,11},{10,... | collective-permute-start | bytes 393224 | tf_op jit(solution)/shard_map/while/body/eval_jaxpr/ppermute | solution.py:41
  67.8 6.3 %collective-permute-done.1 = f32[2,64,256]{2,1,0:T(8,128)S(1)} collective-permute-done((f32[2,64,256]{2,1,0:T(8,128)S(1)}, f32[2,64,256]{2,1,0:T(8,128)S(1)}, u32[]{:S(2)}, u32[]{:S(2)}) %collective-permute-start.1) | collective-permute-done | bytes 131104 | tf_op jit(solution)/shard_map/while/body/eval_jaxpr/ppermute | solution.py:41
  75.3 8.3 %all-gather.2 = bf16[8,64,256]{2,1,0:T(8,128)(2,1)S(1)} all-gather(bf16[1,64,256]{2,1,0:T(8,128)(2,1)S(1)} %dynamic-slice_multiply_fusion.2), channel_id=2, replica_groups=mesh['prow'=8,'pcol'=4] {'prow'}, dimensions={0}, use_global_device_ids=true | all-gather | bytes 294912 | tf_op jit(solution)/shard_map/while/body/eval_jaxpr/all_gather | solution.py:51
  86.8 5.1 %collective-permute-done = f32[2,64,256]{2,1,0:T(8,128)S(1)} collective-permute-done((f32[2,64,256]{2,1,0:T(8,128)S(1)}, f32[2,64,256]{2,1,0:T(8,128)S(1)}, u32[]{:S(2)}, u32[]{:S(2)}) %collective-permute-start) | collective-permute-done | bytes 131104 | tf_op jit(solution)/shard_map/while/body/eval_jaxpr/ppermute | solution.py:41
  91.9 2.4 %collective-permute-start.1 = (f32[2,64,256]{2,1,0:T(8,128)S(1)}, f32[2,64,256]{2,1,0:T(8,128)S(1)}, u32[]{:S(2)}, u32[]{:S(2)}) collective-permute-start(f32[2,64,256]{2,1,0:T(8,128)S(1)} %add.164), channel_id=1, source_target_pairs={{0,2},{1,3},{2,0},{3,1},{4,6},{5,7},{6,4},{7,5},{8,10},{9,11},{10,... | collective-permute-start | bytes 393224 | tf_op jit(solution)/shard_map/while/body/eval_jaxpr/ppermute | solution.py:41
  94.2 6.3 %collective-permute-done.1 = f32[2,64,256]{2,1,0:T(8,128)S(1)} collective-permute-done((f32[2,64,256]{2,1,0:T(8,128)S(1)}, f32[2,64,256]{2,1,0:T(8,128)S(1)}, u32[]{:S(2)}, u32[]{:S(2)}) %collective-permute-start.1) | collective-permute-done | bytes 131104 | tf_op jit(solution)/shard_map/while/body/eval_jaxpr/ppermute | solution.py:41
  101.7 9.3 %all-gather.2 = bf16[8,64,256]{2,1,0:T(8,128)(2,1)S(1)} all-gather(bf16[1,64,256]{2,1,0:T(8,128)(2,1)S(1)} %dynamic-slice_multiply_fusion.2), channel_id=2, replica_groups=mesh['prow'=8,'pcol'=4] {'prow'}, dimensions={0}, use_global_device_ids=true | all-gather | bytes 294912 | tf_op jit(solution)/shard_map/while/body/eval_jaxpr/all_gather | solution.py:51
  114.2 5.1 %collective-permute-done = f32[2,64,256]{2,1,0:T(8,128)S(1)} collective-permute-done((f32[2,64,256]{2,1,0:T(8,128)S(1)}, f32[2,64,256]{2,1,0:T(8,128)S(1)}, u32[]{:S(2)}, u32[]{:S(2)}) %collective-permute-start) | collective-permute-done | bytes 131104 | tf_op jit(solution)/shard_map/while/body/eval_jaxpr/ppermute | solution.py:41
  121.7 6.3 %collective-permute-done.1 = f32[2,64,256]{2,1,0:T(8,128)S(1)} collective-permute-done((f32[2,64,256]{2,1,0:T(8,128)S(1)}, f32[2,64,256]{2,1,0:T(8,128)S(1)}, u32[]{:S(2)}, u32[]{:S(2)}) %collective-permute-start.1) | collective-permute-done | bytes 131104 | tf_op jit(solution)/shard_map/while/body/eval_jaxpr/ppermute | solution.py:41
  129.2 8.3 %all-gather.2 = bf16[8,64,256]{2,1,0:T(8,128)(2,1)S(1)} all-gather(bf16[1,64,256]{2,1,0:T(8,128)(2,1)S(1)} %dynamic-slice_multiply_fusion.2), channel_id=2, replica_groups=mesh['prow'=8,'pcol'=4] {'prow'}, dimensions={0}, use_global_device_ids=true | all-gather | bytes 294912 | tf_op jit(solution)/shard_map/while/body/eval_jaxpr/all_gather | solution.py:51
  140.7 5.1 %collective-permute-done = f32[2,64,256]{2,1,0:T(8,128)S(1)} collective-permute-done((f32[2,64,256]{2,1,0:T(8,128)S(1)}, f32[2,64,256]{2,1,0:T(8,128)S(1)}, u32[]{:S(2)}, u32[]{:S(2)}) %collective-permute-start) | collective-permute-done | bytes 131104 | tf_op jit(solution)/shard_map/while/body/eval_jaxpr/ppermute | solution.py:41
  145.8 2.4 %collective-permute-start.1 = (f32[2,64,256]{2,1,0:T(8,128)S(1)}, f32[2,64,256]{2,1,0:T(8,128)S(1)}, u32[]{:S(2)}, u32[]{:S(2)}) collective-permute-start(f32[2,64,256]{2,1,0:T(8,128)S(1)} %add.164), channel_id=1, source_target_pairs={{0,2},{1,3},{2,0},{3,1},{4,6},{5,7},{6,4},{7,5},{8,10},{9,11},{10,... | collective-permute-start | bytes 393224 | tf_op jit(solution)/shard_map/while/body/eval_jaxpr/ppermute | solution.py:41
  148.2 6.3 %collective-permute-done.1 = f32[2,64,256]{2,1,0:T(8,128)S(1)} collective-permute-done((f32[2,64,256]{2,1,0:T(8,128)S(1)}, f32[2,64,256]{2,1,0:T(8,128)S(1)}, u32[]{:S(2)}, u32[]{:S(2)}) %collective-permute-start.1) | collective-permute-done | bytes 131104 | tf_op jit(solution)/shard_map/while/body/eval_jaxpr/ppermute | solution.py:41
  155.7 9.3 %all-gather.2 = bf16[8,64,256]{2,1,0:T(8,128)(2,1)S(1)} all-gather(bf16[1,64,256]{2,1,0:T(8,128)(2,1)S(1)} %dynamic-slice_multiply_fusion.2), channel_id=2, replica_groups=mesh['prow'=8,'pcol'=4] {'prow'}, dimensions={0}, use_global_device_ids=true | all-gather | bytes 294912 | tf_op jit(solution)/shard_map/while/body/eval_jaxpr/all_gather | solution.py:51
  168.1 5.1 %collective-permute-done = f32[2,64,256]{2,1,0:T(8,128)S(1)} collective-permute-done((f32[2,64,256]{2,1,0:T(8,128)S(1)}, f32[2,64,256]{2,1,0:T(8,128)S(1)}, u32[]{:S(2)}, u32[]{:S(2)}) %collective-permute-start) | collective-permute-done | bytes 131104 | tf_op jit(solution)/shard_map/while/body/eval_jaxpr/ppermute | solution.py:41
  175.6 6.3 %collective-permute-done.1 = f32[2,64,256]{2,1,0:T(8,128)S(1)} collective-permute-done((f32[2,64,256]{2,1,0:T(8,128)S(1)}, f32[2,64,256]{2,1,0:T(8,128)S(1)}, u32[]{:S(2)}, u32[]{:S(2)}) %collective-permute-start.1) | collective-permute-done | bytes 131104 | tf_op jit(solution)/shard_map/while/body/eval_jaxpr/ppermute | solution.py:41
  183.1 8.3 %all-gather.2 = bf16[8,64,256]{2,1,0:T(8,128)(2,1)S(1)} all-gather(bf16[1,64,256]{2,1,0:T(8,128)(2,1)S(1)} %dynamic-slice_multiply_fusion.2), channel_id=2, replica_groups=mesh['prow'=8,'pcol'=4] {'prow'}, dimensions={0}, use_global_device_ids=true | all-gather | bytes 294912 | tf_op jit(solution)/shard_map/while/body/eval_jaxpr/all_gather | solution.py:51
  194.6 5.1 %collective-permute-done = f32[2,64,256]{2,1,0:T(8,128)S(1)} collective-permute-done((f32[2,64,256]{2,1,0:T(8,128)S(1)}, f32[2,64,256]{2,1,0:T(8,128)S(1)}, u32[]{:S(2)}, u32[]{:S(2)}) %collective-permute-start) | collective-permute-done | bytes 131104 | tf_op jit(solution)/shard_map/while/body/eval_jaxpr/ppermute | solution.py:41
  199.7 2.4 %collective-permute-start.1 = (f32[2,64,256]{2,1,0:T(8,128)S(1)}, f32[2,64,256]{2,1,0:T(8,128)S(1)}, u32[]{:S(2)}, u32[]{:S(2)}) collective-permute-start(f32[2,64,256]{2,1,0:T(8,128)S(1)} %add.164), channel_id=1, source_target_pairs={{0,2},{1,3},{2,0},{3,1},{4,6},{5,7},{6,4},{7,5},{8,10},{9,11},{10,... | collective-permute-start | bytes 393224 | tf_op jit(solution)/shard_map/while/body/eval_jaxpr/ppermute | solution.py:41
  202.1 6.3 %collective-permute-done.1 = f32[2,64,256]{2,1,0:T(8,128)S(1)} collective-permute-done((f32[2,64,256]{2,1,0:T(8,128)S(1)}, f32[2,64,256]{2,1,0:T(8,128)S(1)}, u32[]{:S(2)}, u32[]{:S(2)}) %collective-permute-start.1) | collective-permute-done | bytes 131104 | tf_op jit(solution)/shard_map/while/body/eval_jaxpr/ppermute | solution.py:41
  209.6 9.3 %all-gather.2 = bf16[8,64,256]{2,1,0:T(8,128)(2,1)S(1)} all-gather(bf16[1,64,256]{2,1,0:T(8,128)(2,1)S(1)} %dynamic-slice_multiply_fusion.2), channel_id=2, replica_groups=mesh['prow'=8,'pcol'=4] {'prow'}, dimensions={0}, use_global_device_ids=true | all-gather | bytes 294912 | tf_op jit(solution)/shard_map/while/body/eval_jaxpr/all_gather | solution.py:51
  (95 shorter events, 41.3 us)
Async XLA Ops:
  4.2 6.6 %collective-permute-start = (f32[2,64,256]{2,1,0:T(8,128)S(1)}, f32[2,64,256]{2,1,0:T(8,128)S(1)}, u32[]{:S(2)}, u32[]{:S(2)}) collective-permute-start(f32[2,64,256]{2,1,0:T(8,128)S(1)} %convolution_bitcast_fusion.2), channel_id=1, source_target_pairs={{0,1},{1,0},{2,3},{3,2},{4,5},{5,4},{6,7},{7,6},{8,9},{9,8},{10,11... | collective-permute-start | bytes 393224 | tf_op jit(solution)/shard_map/while/body/eval_jaxpr/ppermute | solution.py:41
  10.8 8.4 %collective-permute-start.1 = (f32[2,64,256]{2,1,0:T(8,128)S(1)}, f32[2,64,256]{2,1,0:T(8,128)S(1)}, u32[]{:S(2)}, u32[]{:S(2)}) collective-permute-start(f32[2,64,256]{2,1,0:T(8,128)S(1)} %add.164), channel_id=1, source_target_pairs={{0,2},{1,3},{2,0},{3,1},{4,6},{5,7},{6,4},{7,5},{8,10},{9,11},{10,... | collective-permute-start | bytes 393224 | tf_op jit(solution)/shard_map/while/body/eval_jaxpr/ppermute | solution.py:41
  32.1 5.8 %collective-permute-start = (f32[2,64,256]{2,1,0:T(8,128)S(1)}, f32[2,64,256]{2,1,0:T(8,128)S(1)}, u32[]{:S(2)}, u32[]{:S(2)}) collective-permute-start(f32[2,64,256]{2,1,0:T(8,128)S(1)} %convolution_bitcast_fusion.2), channel_id=1, source_target_pairs={{0,1},{1,0},{2,3},{3,2},{4,5},{5,4},{6,7},{7,6},{8,9},{9,8},{10,11... | collective-permute-start | bytes 393224 | tf_op jit(solution)/shard_map/while/body/eval_jaxpr/ppermute | solution.py:41
  37.9 8.7 %collective-permute-start.1 = (f32[2,64,256]{2,1,0:T(8,128)S(1)}, f32[2,64,256]{2,1,0:T(8,128)S(1)}, u32[]{:S(2)}, u32[]{:S(2)}) collective-permute-start(f32[2,64,256]{2,1,0:T(8,128)S(1)} %add.164), channel_id=1, source_target_pairs={{0,2},{1,3},{2,0},{3,1},{4,6},{5,7},{6,4},{7,5},{8,10},{9,11},{10,... | collective-permute-start | bytes 393224 | tf_op jit(solution)/shard_map/while/body/eval_jaxpr/ppermute | solution.py:41
  59.5 5.8 %collective-permute-start = (f32[2,64,256]{2,1,0:T(8,128)S(1)}, f32[2,64,256]{2,1,0:T(8,128)S(1)}, u32[]{:S(2)}, u32[]{:S(2)}) collective-permute-start(f32[2,64,256]{2,1,0:T(8,128)S(1)} %convolution_bitcast_fusion.2), channel_id=1, source_target_pairs={{0,1},{1,0},{2,3},{3,2},{4,5},{5,4},{6,7},{7,6},{8,9},{9,8},{10,11... | collective-permute-start | bytes 393224 | tf_op jit(solution)/shard_map/while/body/eval_jaxpr/ppermute | solution.py:41
  65.4 8.7 %collective-permute-start.1 = (f32[2,64,256]{2,1,0:T(8,128)S(1)}, f32[2,64,256]{2,1,0:T(8,128)S(1)}, u32[]{:S(2)}, u32[]{:S(2)}) collective-permute-start(f32[2,64,256]{2,1,0:T(8,128)S(1)} %add.164), channel_id=1, source_target_pairs={{0,2},{1,3},{2,0},{3,1},{4,6},{5,7},{6,4},{7,5},{8,10},{9,11},{10,... | collective-permute-start | bytes 393224 | tf_op jit(solution)/shard_map/while/body/eval_jaxpr/ppermute | solution.py:41
  86.0 5.8 %collective-permute-start = (f32[2,64,256]{2,1,0:T(8,128)S(1)}, f32[2,64,256]{2,1,0:T(8,128)S(1)}, u32[]{:S(2)}, u32[]{:S(2)}) collective-permute-start(f32[2,64,256]{2,1,0:T(8,128)S(1)} %convolution_bitcast_fusion.2), channel_id=1, source_target_pairs={{0,1},{1,0},{2,3},{3,2},{4,5},{5,4},{6,7},{7,6},{8,9},{9,8},{10,11... | collective-permute-start | bytes 393224 | tf_op jit(solution)/shard_map/while/body/eval_jaxpr/ppermute | solution.py:41
  91.9 8.7 %collective-permute-start.1 = (f32[2,64,256]{2,1,0:T(8,128)S(1)}, f32[2,64,256]{2,1,0:T(8,128)S(1)}, u32[]{:S(2)}, u32[]{:S(2)}) collective-permute-start(f32[2,64,256]{2,1,0:T(8,128)S(1)} %add.164), channel_id=1, source_target_pairs={{0,2},{1,3},{2,0},{3,1},{4,6},{5,7},{6,4},{7,5},{8,10},{9,11},{10,... | collective-permute-start | bytes 393224 | tf_op jit(solution)/shard_map/while/body/eval_jaxpr/ppermute | solution.py:41
  113.5 5.8 %collective-permute-start = (f32[2,64,256]{2,1,0:T(8,128)S(1)}, f32[2,64,256]{2,1,0:T(8,128)S(1)}, u32[]{:S(2)}, u32[]{:S(2)}) collective-permute-start(f32[2,64,256]{2,1,0:T(8,128)S(1)} %convolution_bitcast_fusion.2), channel_id=1, source_target_pairs={{0,1},{1,0},{2,3},{3,2},{4,5},{5,4},{6,7},{7,6},{8,9},{9,8},{10,11... | collective-permute-start | bytes 393224 | tf_op jit(solution)/shard_map/while/body/eval_jaxpr/ppermute | solution.py:41
  119.3 8.7 %collective-permute-start.1 = (f32[2,64,256]{2,1,0:T(8,128)S(1)}, f32[2,64,256]{2,1,0:T(8,128)S(1)}, u32[]{:S(2)}, u32[]{:S(2)}) collective-permute-start(f32[2,64,256]{2,1,0:T(8,128)S(1)} %add.164), channel_id=1, source_target_pairs={{0,2},{1,3},{2,0},{3,1},{4,6},{5,7},{6,4},{7,5},{8,10},{9,11},{10,... | collective-permute-start | bytes 393224 | tf_op jit(solution)/shard_map/while/body/eval_jaxpr/ppermute | solution.py:41
  139.9 5.8 %collective-permute-start = (f32[2,64,256]{2,1,0:T(8,128)S(1)}, f32[2,64,256]{2,1,0:T(8,128)S(1)}, u32[]{:S(2)}, u32[]{:S(2)}) collective-permute-start(f32[2,64,256]{2,1,0:T(8,128)S(1)} %convolution_bitcast_fusion.2), channel_id=1, source_target_pairs={{0,1},{1,0},{2,3},{3,2},{4,5},{5,4},{6,7},{7,6},{8,9},{9,8},{10,11... | collective-permute-start | bytes 393224 | tf_op jit(solution)/shard_map/while/body/eval_jaxpr/ppermute | solution.py:41
  145.8 8.7 %collective-permute-start.1 = (f32[2,64,256]{2,1,0:T(8,128)S(1)}, f32[2,64,256]{2,1,0:T(8,128)S(1)}, u32[]{:S(2)}, u32[]{:S(2)}) collective-permute-start(f32[2,64,256]{2,1,0:T(8,128)S(1)} %add.164), channel_id=1, source_target_pairs={{0,2},{1,3},{2,0},{3,1},{4,6},{5,7},{6,4},{7,5},{8,10},{9,11},{10,... | collective-permute-start | bytes 393224 | tf_op jit(solution)/shard_map/while/body/eval_jaxpr/ppermute | solution.py:41
  167.4 5.8 %collective-permute-start = (f32[2,64,256]{2,1,0:T(8,128)S(1)}, f32[2,64,256]{2,1,0:T(8,128)S(1)}, u32[]{:S(2)}, u32[]{:S(2)}) collective-permute-start(f32[2,64,256]{2,1,0:T(8,128)S(1)} %convolution_bitcast_fusion.2), channel_id=1, source_target_pairs={{0,1},{1,0},{2,3},{3,2},{4,5},{5,4},{6,7},{7,6},{8,9},{9,8},{10,11... | collective-permute-start | bytes 393224 | tf_op jit(solution)/shard_map/while/body/eval_jaxpr/ppermute | solution.py:41
  173.2 8.7 %collective-permute-start.1 = (f32[2,64,256]{2,1,0:T(8,128)S(1)}, f32[2,64,256]{2,1,0:T(8,128)S(1)}, u32[]{:S(2)}, u32[]{:S(2)}) collective-permute-start(f32[2,64,256]{2,1,0:T(8,128)S(1)} %add.164), channel_id=1, source_target_pairs={{0,2},{1,3},{2,0},{3,1},{4,6},{5,7},{6,4},{7,5},{8,10},{9,11},{10,... | collective-permute-start | bytes 393224 | tf_op jit(solution)/shard_map/while/body/eval_jaxpr/ppermute | solution.py:41
  193.9 5.8 %collective-permute-start = (f32[2,64,256]{2,1,0:T(8,128)S(1)}, f32[2,64,256]{2,1,0:T(8,128)S(1)}, u32[]{:S(2)}, u32[]{:S(2)}) collective-permute-start(f32[2,64,256]{2,1,0:T(8,128)S(1)} %convolution_bitcast_fusion.2), channel_id=1, source_target_pairs={{0,1},{1,0},{2,3},{3,2},{4,5},{5,4},{6,7},{7,6},{8,9},{9,8},{10,11... | collective-permute-start | bytes 393224 | tf_op jit(solution)/shard_map/while/body/eval_jaxpr/ppermute | solution.py:41
  199.7 8.7 %collective-permute-start.1 = (f32[2,64,256]{2,1,0:T(8,128)S(1)}, f32[2,64,256]{2,1,0:T(8,128)S(1)}, u32[]{:S(2)}, u32[]{:S(2)}) collective-permute-start(f32[2,64,256]{2,1,0:T(8,128)S(1)} %add.164), channel_id=1, source_target_pairs={{0,2},{1,3},{2,0},{3,1},{4,6},{5,7},{6,4},{7,5},{8,10},{9,11},{10,... | collective-permute-start | bytes 393224 | tf_op jit(solution)/shard_map/while/body/eval_jaxpr/ppermute | solution.py:41
  218.9 0.8 copy-start
